TPU v7x, 256 devices: a whole 4x4x8 slice. The times are simulated.
256 devices in a mesh: seq: 32 (over y, z), head: 8 (over x, core).
Axes of the slice: x: 4, y: 4, z: 8, core: 2. Of those that a mesh axis runs over, the one named last changes fastest.
Arguments:
- doc_lengths: int32 [256], P(('seq', 'head')), may hold values from 1 to 2688, 24576 in all
- queries: bfloat16 [24576, 8192], P('seq', 'head'), may hold values from -24 to 24
- key_states: bfloat16 [24576, 1024], P('seq', 'head'), may hold values from -24 to 24
- value_states: bfloat16 [24576, 1024], P('seq', 'head'), may hold values from -6 to 6
Outputs:
- attended: bfloat16 [24576, 8192], P('seq', 'head')
Inputs may be any that keep to these rules, and one draw needn't show every extreme that they name: `doc_lengths`: the 256 lengths sum to 24576; the largest is exactly 2688.
All inputs are finite; a program needn't handle non-finite values. No bound on the sum of `doc_lengths` on one device may be relied on, other than what follows from the above.
Results may differ from a plain program's by a relative error of at most 0.0028.
Values may be sent and summed in bfloat16 or wider, within the bound.
A program may use at most 64 MiB of HBM per device.

v0:
```python
import functools
import math

import jax
import jax.numpy as jnp
from jax import lax
from jax.experimental import pallas as pl
from jax.experimental.pallas import tpu as pltpu
from jax.sharding import PartitionSpec as P

HD = 128
TILE = 128
HALF_HEADS = 4
Z = 8
Y = 4
X = 8
LOG2_SCALE = math.log2(math.e) / math.sqrt(HD)
HIDDEN = -1e30
MESH = pl.DeviceIdType.MESH


def exchange_partners(seq, head):
    y, z = seq // Z, seq % Z
    ring_z = [(y * Z + (z + k) % Z, head) for k in range(1, Z)]
    ring_y = [(((y + k) % Y) * Z + z, head) for k in range(1, Y)]
    ring_x = [(seq, (head + k) % X) for k in range(1, X)]
    return ring_z, ring_y, ring_x


def kernel(
    len_ref, q_hbm, k_hbm, v_hbm, out_ref,
    q_buf, k_buf, v_buf, own_len, len_z, len_y, len_x,
    q_extra, k_extra, starts, bias, scores_a, scores_b, row_max, acc,
    load_sems, send_sems, recv_sems, len_send, len_recv,
):
    rows = q_hbm.shape[0]
    half = rows // 2
    tiles = rows // TILE
    devices = 32
    seq = lax.axis_index("seq")
    head = lax.axis_index("head")
    y, z = seq // Z, seq % Z
    following = (lax.rem(seq + 1, devices), head)
    previous = (lax.rem(seq + devices - 1, devices), head)
    ring_z, ring_y, ring_x = exchange_partners(seq, head)

    load_k = pltpu.make_async_copy(k_hbm, k_buf.at[0], load_sems.at[0])
    load_v = pltpu.make_async_copy(v_hbm, v_buf.at[0], load_sems.at[1])
    load_q = pltpu.make_async_copy(q_hbm, q_buf, load_sems.at[2])
    load_k.start()
    load_v.start()
    load_q.start()
    length = jnp.full((1, 1, 128), len_ref[0], jnp.int32)
    own_len[...] = length
    len_z[pl.ds(z, 1)] = length

    barrier = pltpu.get_barrier_semaphore()
    partners = ring_z + ring_y + ring_x + [following, previous]
    for partner in partners:
        pl.semaphore_signal(barrier, inc=1, device_id=partner, device_id_type=MESH)
    pl.semaphore_wait(barrier, len(partners))

    def sends(source, target, partners_of, base):
        return [
            pltpu.make_async_remote_copy(
                src_ref=source, dst_ref=target,
                send_sem=len_send.at[base + n], recv_sem=len_recv.at[base + n],
                device_id=partner, device_id_type=MESH,
            )
            for n, partner in enumerate(partners_of)
        ]

    def hop(slot, part):
        copies = []
        for n, buf in enumerate((k_buf, v_buf)):
            ref = buf.at[slot, pl.ds(part * half, half)]
            if slot == 3:
                target = buf.at[4, pl.ds(0, half)]
            else:
                target = buf.at[slot + 1, pl.ds(part * half, half)]
            copies.append(
                pltpu.make_async_remote_copy(
                    src_ref=ref, dst_ref=target,
                    send_sem=send_sems.at[slot, part, n],
                    recv_sem=recv_sems.at[slot, part, n],
                    device_id=following, device_id_type=MESH,
                )
            )
        return copies

    hops = {(slot, part): hop(slot, part) for slot in range(4) for part in range(slot == 3, 2)}

    def start_hop(slot, part):
        for copy in hops[slot, part]:
            copy.start()

    def wait_hop(slot, part):
        for copy in hops[slot, part]:
            copy.wait_recv()

    z_sends = sends(own_len, len_z.at[pl.ds(z, 1)], ring_z, 0)
    for copy in z_sends:
        copy.start()
    load_k.wait()
    load_v.wait()
    start_hop(0, 0)
    start_hop(0, 1)
    for copy in z_sends:
        copy.wait_recv()
    len_y[pl.ds(y, 1)] = len_z[...].reshape(1, Z, 1, 128)
    y_sends = sends(len_z, len_y.at[y], ring_y, Z - 1)
    for copy in y_sends:
        copy.start()
    wait_hop(0, 0)
    start_hop(1, 0)
    for copy in y_sends:
        copy.wait_recv()
    x_sends = sends(len_y, len_x.at[head], ring_x, Z - 1 + Y - 1)
    for copy in x_sends:
        copy.start()
    len_x[pl.ds(head, 1)] = len_y[...].reshape(1, Y, Z, 1, 128)
    wait_hop(0, 1)
    start_hop(1, 1)
    load_q.wait()
    for copy in x_sends:
        copy.wait_recv()

    lane = lax.broadcasted_iota(jnp.int32, (1, 128), 1)

    def add_lengths(n, ends):
        low, high = ends
        for m in range(X):
            length_row = len_x[m, n // Z, n % Z]
            doc = n * X + m
            low = low + jnp.where(lane >= doc, length_row, 0)
            high = high + jnp.where(lane + 128 >= doc, length_row, 0)
        return low, high

    zero_row = jnp.zeros((1, 128), jnp.int32)
    low, high = lax.fori_loop(0, devices, add_lengths, (zero_row, zero_row))
    ends = jnp.concatenate([low, high], axis=1)
    first = seq * rows
    doc_first = jnp.max(jnp.where(ends <= first, ends, 0), axis=1, keepdims=True)
    doc_end = jnp.min(jnp.where(ends > first, ends, 1 << 30), axis=1, keepdims=True)
    column = lax.broadcasted_iota(jnp.int32, (TILE, 128), 0)
    lanes = lax.broadcasted_iota(jnp.int32, (TILE, 128), 1)

    def tile_masks(tile, carry):
        at = pl.ds(tile * TILE, TILE)
        position = first + tile * TILE + column
        done = jnp.where(ends <= position[:, :1], ends, 0)
        starts[at, :] = jnp.broadcast_to(jnp.max(done, axis=1, keepdims=True), (TILE, 128)) - first
        later = jnp.where(position >= doc_end, 1.0, 0.0)
        q_extra[at, :] = jnp.where(lanes == 0, later, jnp.where(lanes == 1, 1.0, 0.0)).astype(jnp.bfloat16)
        for slot in range(1, 5):
            token = position - slot * rows
            before = jnp.where(token < doc_first, HIDDEN, 0.0)
            k_extra[slot, at, :] = jnp.where(
                lanes == 0, HIDDEN, jnp.where(lanes == 1, before, 0.0)
            ).astype(jnp.bfloat16)
        return carry

    lax.fori_loop(0, tiles, tile_masks, 0)

    def queries_of(tile, group, own):
        at = pl.ds(tile * TILE, TILE)
        parts = []
        for n in range(HALF_HEADS):
            cols = pl.ds((group * HALF_HEADS + n) * HD, HD)
            parts.append(q_buf[at, cols])
        stacked = jnp.concatenate(parts, axis=0)
        if own:
            return stacked
        extra = jnp.concatenate([q_extra[at, :]] * HALF_HEADS, axis=0)
        return jnp.concatenate([stacked, extra], axis=1)

    def attend(slot, tile_range, key0, width, hooks):
        own = slot == 0
        keys_at = pl.ds(key0, width)
        extra0 = half if slot == 4 else 0

        def score(tile, group, target):
            keys = k_buf[slot, keys_at, :]
            if not own:
                extra = k_extra[slot, pl.ds(extra0 + key0, width), :]
                keys = jnp.concatenate([keys, extra], axis=1)
            target[:, pl.ds(0, width)] = lax.dot_general(
                queries_of(tile, group, own), keys, (((1,), (1,)), ((), ())),
                preferred_element_type=jnp.float32,
            )

        def combine(tile, group, source):
            parts, shrinks = [], []
            for n in range(HALF_HEADS):
                s = source[pl.ds(n * TILE, TILE), pl.ds(0, width)]
                at = pl.ds(n * TILE, TILE)
                if own:
                    s = s + bias[:, pl.ds(0, width)]
                    top = jnp.max(s, axis=1, keepdims=True)
                else:
                    old = row_max[tile, group, at, :]
                    top = jnp.maximum(old, jnp.max(s, axis=1, keepdims=True))
                    shrinks.append(jnp.exp2((old - top) * LOG2_SCALE))
                row_max[tile, group, at, :] = jnp.broadcast_to(top, (TILE, 128))
                if not own:
                    top = jnp.concatenate([top] * (width // 128), axis=1)
                parts.append(jnp.exp2((s - top) * LOG2_SCALE).astype(jnp.bfloat16))
            values = jnp.concatenate(
                [v_buf[slot, keys_at, :], jnp.ones((width, 128), jnp.bfloat16)], axis=1
            )
            update = jnp.dot(
                jnp.concatenate(parts, axis=0), values, preferred_element_type=jnp.float32
            )
            if own:
                acc[tile, group] = update
            else:
                shrink = jnp.concatenate(shrinks, axis=0)
                shrink = jnp.concatenate([shrink, shrink], axis=1)
                acc[tile, group] = acc[tile, group] * shrink + update

        begin, end = tile_range
        score(begin, 0, scores_a)

        def step(tile, carry):
            for at_tile, hook in hooks.items():
                pl.when(tile == at_tile)(hook)
            if own:
                token = lax.broadcasted_iota(jnp.int32, (TILE, width), 1) + key0
                mine = tile * TILE + lax.broadcasted_iota(jnp.int32, (TILE, width), 0)
                begins = starts[pl.ds(tile * TILE, TILE), :]
                begins = jnp.concatenate([begins] * (width // 128), axis=1)
                seen = (token >= begins) & (token <= mine)
                bias[:, pl.ds(0, width)] = jnp.where(seen, 0.0, HIDDEN)
            score(tile, 1, scores_b)
            combine(tile, 0, scores_a)
            score(jnp.minimum(tile + 1, end - 1), 0, scores_a)
            combine(tile, 1, scores_b)
            return carry

        lax.fori_loop(begin, end, step, 0)

    def forward(slot, part):
        def run():
            wait_hop(slot, part)
            if (slot + 1, part) in hops:
                start_hop(slot + 1, part)
        return run

    for pair in range(tiles // 2):
        attend(0, (2 * pair, 2 * pair + 2), 0, 2 * TILE * (pair + 1), {})
    forward(1, 0)()
    attend(1, (0, tiles), 0, rows, {4: forward(1, 1)})
    attend(2, (0, tiles), 0, rows, {4: forward(2, 0)})
    forward(2, 1)()
    attend(3, (0, tiles), 0, rows, {})
    forward(3, 1)()
    attend(4, (0, tiles // 2), 0, half, {})

    def finish(tile, carry):
        for group in range(2):
            done = acc[tile, group]
            done = (done[:, :HD] / done[:, HD:]).astype(jnp.bfloat16)
            for n in range(HALF_HEADS):
                cols = pl.ds((group * HALF_HEADS + n) * HD, HD)
                out_ref[pl.ds(tile * TILE, TILE), cols] = done[n * TILE : (n + 1) * TILE]
        return carry

    lax.fori_loop(0, tiles, finish, 0)
    for copy in z_sends + y_sends + x_sends:
        copy.wait_send()
    for copies in hops.values():
        for copy in copies:
            copy.wait_send()


def body(doc_lengths, queries, key_states, value_states):
    rows, cols = queries.shape
    tiles = rows // TILE
    group_rows = HALF_HEADS * TILE
    vmem = pltpu.VMEM
    any_space = pl.BlockSpec(memory_space=pl.ANY)
    return pl.pallas_call(
        kernel,
        out_shape=jax.ShapeDtypeStruct((rows, cols), jnp.bfloat16),
        in_specs=[pl.BlockSpec(memory_space=pltpu.SMEM), any_space, any_space, any_space],
        out_specs=pl.BlockSpec(memory_space=pltpu.VMEM),
        scratch_shapes=[
            vmem((rows, cols), jnp.bfloat16),
            vmem((5, rows, HD), jnp.bfloat16),
            vmem((5, rows, HD), jnp.bfloat16),
            vmem((1, 1, 128), jnp.int32),
            vmem((Z, 1, 128), jnp.int32),
            vmem((Y, Z, 1, 128), jnp.int32),
            vmem((X, Y, Z, 1, 128), jnp.int32),
            vmem((rows, 128), jnp.bfloat16),
            vmem((5, rows, 128), jnp.bfloat16),
            vmem((rows, 128), jnp.int32),
            vmem((TILE, rows), jnp.float32),
            vmem((group_rows, rows), jnp.float32),
            vmem((group_rows, rows), jnp.float32),
            vmem((tiles, 2, group_rows, 128), jnp.float32),
            vmem((tiles, 2, group_rows, 2 * HD), jnp.float32),
            pltpu.SemaphoreType.DMA((3,)),
            pltpu.SemaphoreType.DMA((4, 2, 2)),
            pltpu.SemaphoreType.DMA((4, 2, 2)),
            pltpu.SemaphoreType.DMA((Z + Y + X - 3,)),
            pltpu.SemaphoreType.DMA((Z + Y + X - 3,)),
        ],
        compiler_params=pltpu.CompilerParams(
            collective_id=0, has_side_effects=True, vmem_limit_bytes=56 * 1024 * 1024
        ),
    )(doc_lengths, queries, key_states, value_states)


def solution(mesh):
    return jax.shard_map(
        body,
        mesh=mesh,
        in_specs=(P(("seq", "head")), P("seq", "head"), P("seq", "head"), P("seq", "head")),
        out_specs=P("seq", "head"),
        check_vma=False,
    )
```

profile of v0, /device:TPU:1, one launch (start us, length us, event | category | flops | bytes accessed | tf_op | source)
XLA Modules:
  0.0 74.3 jit_solution(10074293325419714660)
XLA Ops:
  0.7 70.9 %shard_map.46 = bf16[768,1024]{1,0:T(8,128)(2,1)} custom-call(s32[1]{0:T(128)S(6)} %copy.6.len_ref, bf16[768,1024]{1,0:T(8,128)(2,1)} %q_hbm.1, bf16[768,128]{1,0:T(8,128)(2,1)} %k_hbm.1, bf16[768,128]{1,0:T(8,128)(2,1)} %v_hbm.1), custom_call_target="tpu_custom_call" | custom-call | tf_op jit(solution)/shard_map/pallas_call | solution.py:282
  71.6 2.7 %copy.7 = bf16[768,1024]{1,0:T(8,128)(2,1)} copy(bf16[768,1024]{1,0:T(8,128)(2,1)} %shard_map.46) | data formatting | bytes 3145728
where the time goes:
time: 74.4 us; the launch traced here: 74.3 us
  Pallas kernels  70.9 us (95%)
  local copies, waits for them, and re-layouts  2.67 us (4%)
    pallas_call x1, Pallas kernels, body(): pl.pallas_call(kernel, out_shape=jax.ShapeDtypeStruct((rows, cols), jnp.b...  70.9 us
    unnamed x1, local copies, waits for them, and re-layouts  2.67 us

commit v1 on v0

v1 whole, which is shorter than its diff:
```python
import functools
import math

import jax
import jax.numpy as jnp
from jax import lax
from jax.experimental import pallas as pl
from jax.experimental.pallas import tpu as pltpu
from jax.sharding import PartitionSpec as P

HD = 128
TILE = 128
HALF_HEADS = 4
SEQ = 32
HEADS = 8
LOG2_SCALE = math.log2(math.e) / math.sqrt(HD)
HIDDEN = -1e30
MESH = pl.DeviceIdType.MESH


def kernel(
    len_ref, q_hbm, k_hbm, v_hbm, acc,
    q_buf, k_buf, v_buf, own_len, len_seq, len_all,
    q_extra, k_extra, starts, bias, scores_a, scores_b, row_max,
    load_sems, send_sems, recv_sems, len_send, len_recv,
):
    rows = q_hbm.shape[0]
    half = rows // 2
    tiles = rows // TILE
    seq = lax.axis_index("seq")
    head = lax.axis_index("head")
    along_seq = [(lax.rem(seq + k, SEQ), head) for k in range(1, SEQ)]
    along_head = [(seq, lax.rem(head + k, HEADS)) for k in range(1, HEADS)]
    following = along_seq[0]

    load_k = pltpu.make_async_copy(k_hbm, k_buf.at[0], load_sems.at[0])
    load_v = pltpu.make_async_copy(v_hbm, v_buf.at[0], load_sems.at[1])
    load_q = pltpu.make_async_copy(q_hbm, q_buf, load_sems.at[2])
    load_k.start()
    load_v.start()
    load_q.start()
    length = jnp.full((1, 1, 128), len_ref[0], jnp.int32)
    own_len[...] = length
    len_seq[pl.ds(seq, 1)] = length

    barrier = pltpu.get_barrier_semaphore()
    partners = along_seq + along_head
    for partner in partners:
        pl.semaphore_signal(barrier, inc=1, device_id=partner, device_id_type=MESH)
    pl.semaphore_wait(barrier, len(partners))

    def sends(source, target, partners_of, base):
        return [
            pltpu.make_async_remote_copy(
                src_ref=source, dst_ref=target,
                send_sem=len_send.at[base + n], recv_sem=len_recv.at[base + n],
                device_id=partner, device_id_type=MESH,
            )
            for n, partner in enumerate(partners_of)
        ]

    def hop(slot, part):
        copies = []
        for n, buf in enumerate((k_buf, v_buf)):
            ref = buf.at[slot, pl.ds(part * half, half)]
            if slot == 3:
                target = buf.at[4, pl.ds(0, half)]
            else:
                target = buf.at[slot + 1, pl.ds(part * half, half)]
            copies.append(
                pltpu.make_async_remote_copy(
                    src_ref=ref, dst_ref=target,
                    send_sem=send_sems.at[slot, part, n],
                    recv_sem=recv_sems.at[slot, part, n],
                    device_id=following, device_id_type=MESH,
                )
            )
        return copies

    hops = {(slot, part): hop(slot, part) for slot in range(4) for part in range(slot == 3, 2)}

    def start_hop(slot, part):
        for copy in hops[slot, part]:
            copy.start()

    def wait_hop(slot, part):
        for copy in hops[slot, part]:
            copy.wait_recv()

    seq_sends = sends(own_len, len_seq.at[pl.ds(seq, 1)], along_seq, 0)
    for copy in seq_sends:
        copy.start()
    load_k.wait()
    load_v.wait()
    start_hop(0, 0)
    start_hop(0, 1)
    for copy in seq_sends:
        copy.wait_recv()
    head_sends = sends(len_seq, len_all.at[head], along_head, SEQ - 1)
    for copy in head_sends:
        copy.start()
    len_all[pl.ds(head, 1)] = len_seq[...].reshape(1, SEQ, 1, 128)
    wait_hop(0, 0)
    start_hop(1, 0)
    load_q.wait()
    for copy in head_sends:
        copy.wait_recv()

    lane = lax.broadcasted_iota(jnp.int32, (1, 128), 1)

    def add_lengths(n, ends):
        low, high = ends
        for m in range(HEADS):
            length_row = len_all[m, n]
            doc = n * HEADS + m
            low = low + jnp.where(lane >= doc, length_row, 0)
            high = high + jnp.where(lane + 128 >= doc, length_row, 0)
        return low, high

    zero_row = jnp.zeros((1, 128), jnp.int32)
    low, high = lax.fori_loop(0, SEQ, add_lengths, (zero_row, zero_row))
    ends = jnp.concatenate([low, high], axis=1)
    first = seq * rows
    doc_first = jnp.max(jnp.where(ends <= first, ends, 0), axis=1, keepdims=True)
    doc_end = jnp.min(jnp.where(ends > first, ends, 1 << 30), axis=1, keepdims=True)
    column = lax.broadcasted_iota(jnp.int32, (TILE, 128), 0)
    lanes = lax.broadcasted_iota(jnp.int32, (TILE, 128), 1)

    def tile_masks(tile, carry):
        at = pl.ds(tile * TILE, TILE)
        position = first + tile * TILE + column
        done = jnp.where(ends <= position[:, :1], ends, 0)
        starts[at, :] = jnp.broadcast_to(jnp.max(done, axis=1, keepdims=True), (TILE, 128)) - first
        later = jnp.where(position >= doc_end, 1.0, 0.0)
        q_extra[at, :] = jnp.where(lanes == 0, later, jnp.where(lanes == 1, 1.0, 0.0)).astype(jnp.bfloat16)
        for slot in range(1, 5):
            token = position - slot * rows
            before = jnp.where(token < doc_first, HIDDEN, 0.0)
            k_extra[slot, at, :] = jnp.where(
                lanes == 0, HIDDEN, jnp.where(lanes == 1, before, 0.0)
            ).astype(jnp.bfloat16)
        return carry

    lax.fori_loop(0, tiles, tile_masks, 0)

    def stacked_queries(tile, group, own):
        at = pl.ds(tile * TILE, TILE)
        parts = []
        for n in range(HALF_HEADS):
            cols = pl.ds((group * HALF_HEADS + n) * HD, HD)
            parts.append(q_buf[at, cols])
        stacked = jnp.concatenate(parts, axis=0)
        if own:
            return stacked
        extra = jnp.concatenate([q_extra[at, :]] * HALF_HEADS, axis=0)
        return jnp.concatenate([stacked, extra], axis=1)

    def score(slot, keys_at, extra_at, tile, group, target):
        own = extra_at is None
        keys = k_buf[slot, keys_at, :]
        if not own:
            keys = jnp.concatenate([keys, k_extra[slot, extra_at, :]], axis=1)
        target[:, pl.ds(0, keys.shape[0])] = lax.dot_general(
            stacked_queries(tile, group, own), keys, (((1,), (1,)), ((), ())),
            preferred_element_type=jnp.float32,
        )

    def combine(slot, keys_at, own, tile, group, source):
        width = keys_at.size
        parts, shrinks = [], []
        for n in range(HALF_HEADS):
            at = pl.ds(n * TILE, TILE)
            s = source[at, pl.ds(0, width)]
            if own:
                s = s + bias[:, pl.ds(0, width)]
                top = jnp.max(s, axis=1, keepdims=True)
            else:
                old = row_max[tile, group, at, :]
                top = jnp.maximum(old, jnp.max(s, axis=1, keepdims=True))
                shrinks.append(jnp.exp2((old - top) * LOG2_SCALE))
            row_max[tile, group, at, :] = jnp.broadcast_to(top, (TILE, 128))
            if not own:
                top = jnp.concatenate([top] * (width // 128), axis=1)
            parts.append(jnp.exp2((s - top) * LOG2_SCALE).astype(jnp.bfloat16))
        values = jnp.concatenate(
            [v_buf[slot, keys_at, :], jnp.ones((width, 128), jnp.bfloat16)], axis=1
        )
        update = jnp.dot(
            jnp.concatenate(parts, axis=0), values, preferred_element_type=jnp.float32
        )
        if own:
            acc[tile, group] = update
        else:
            shrink = jnp.concatenate(shrinks, axis=0)
            shrink = jnp.concatenate([shrink, shrink], axis=1)
            acc[tile, group] = acc[tile, group] * shrink + update

    for pair in range(tiles // 2):
        width = 2 * TILE * (pair + 1)
        keys_at = pl.ds(0, width)
        score(0, keys_at, None, 2 * pair, 0, scores_a)
        for tile in (2 * pair, 2 * pair + 1):
            token = lax.broadcasted_iota(jnp.int32, (TILE, width), 1)
            mine = tile * TILE + lax.broadcasted_iota(jnp.int32, (TILE, width), 0)
            begins = starts[pl.ds(tile * TILE, TILE), :]
            begins = jnp.concatenate([begins] * (width // 128), axis=1)
            seen = (token >= begins) & (token <= mine)
            bias[:, pl.ds(0, width)] = jnp.where(seen, 0.0, HIDDEN)
            score(0, keys_at, None, tile, 1, scores_b)
            combine(0, keys_at, True, tile, 0, scores_a)
            if tile == 2 * pair:
                score(0, keys_at, None, tile + 1, 0, scores_a)
            combine(0, keys_at, True, tile, 1, scores_b)

    def arrived(slot, part):
        wait_hop(slot, part)
        if (slot + 1, part) in hops:
            start_hop(slot + 1, part)

    arrived(0, 1)
    whole = pl.ds(0, rows)
    pairs = tiles // 2
    trips = 3 * pairs

    def place(trip):
        return trip // pairs + 1, trip % pairs * 2

    def trip_body(trip, carry):
        for when, slot, part in ((0, 1, 0), (1, 1, 1), (4, 2, 0), (5, 2, 1)):
            pl.when(trip == when)(functools.partial(arrived, slot, part))
        slot, tile = place(trip)
        next_slot, next_tile = place(jnp.minimum(trip + 1, trips - 1))
        score(slot, whole, whole, tile, 1, scores_b)
        combine(slot, whole, False, tile, 0, scores_a)
        score(slot, whole, whole, tile + 1, 0, scores_a)
        combine(slot, whole, False, tile, 1, scores_b)
        score(slot, whole, whole, tile + 1, 1, scores_b)
        combine(slot, whole, False, tile + 1, 0, scores_a)
        score(next_slot, whole, whole, next_tile, 0, scores_a)
        combine(slot, whole, False, tile + 1, 1, scores_b)
        return carry

    score(1, whole, whole, 0, 0, scores_a)
    lax.fori_loop(0, trips, trip_body, 0)
    arrived(3, 1)
    for tile in range(tiles // 2):
        keys_at = pl.ds(tile * TILE, half - tile * TILE)
        extra_at = pl.ds(half + tile * TILE, half - tile * TILE)
        for group, target in enumerate((scores_a, scores_b)):
            score(4, keys_at, extra_at, tile, group, target)
            combine(4, keys_at, False, tile, group, target)

    for copy in seq_sends + head_sends:
        copy.wait_send()
    for copies in hops.values():
        for copy in copies:
            copy.wait_send()


def finish(acc, out_hbm, out_buf, sems):
    copies = []
    for tile in range(acc.shape[0]):
        at = pl.ds(tile * TILE, TILE)
        for group in range(2):
            done = acc[tile, group]
            done = (done[:, :HD] / done[:, HD:]).astype(jnp.bfloat16)
            for n in range(HALF_HEADS):
                cols = pl.ds((group * HALF_HEADS + n) * HD, HD)
                out_buf[at, cols] = done[n * TILE : (n + 1) * TILE]
        copy = pltpu.make_async_copy(out_buf.at[at], out_hbm.at[at], sems.at[tile])
        copy.start()
        copies.append(copy)
    for copy in copies:
        copy.wait()


def body(doc_lengths, queries, key_states, value_states):
    rows, cols = queries.shape
    tiles = rows // TILE
    group_rows = HALF_HEADS * TILE
    vmem = pltpu.VMEM
    any_space = pl.BlockSpec(memory_space=pl.ANY)
    acc = pl.pallas_call(
        kernel,
        out_shape=vmem((tiles, 2, group_rows, 2 * HD), jnp.float32),
        in_specs=[pl.BlockSpec(memory_space=pltpu.SMEM), any_space, any_space, any_space],
        out_specs=pl.BlockSpec(memory_space=pltpu.VMEM),
        scratch_shapes=[
            vmem((rows, cols), jnp.bfloat16),
            vmem((5, rows, HD), jnp.bfloat16),
            vmem((5, rows, HD), jnp.bfloat16),
            vmem((1, 1, 128), jnp.int32),
            vmem((SEQ, 1, 128), jnp.int32),
            vmem((HEADS, SEQ, 1, 128), jnp.int32),
            vmem((rows, 128), jnp.bfloat16),
            vmem((5, rows, 128), jnp.bfloat16),
            vmem((rows, 128), jnp.int32),
            vmem((TILE, rows), jnp.float32),
            vmem((group_rows, rows), jnp.float32),
            vmem((group_rows, rows), jnp.float32),
            vmem((tiles, 2, group_rows, 128), jnp.float32),
            pltpu.SemaphoreType.DMA((3,)),
            pltpu.SemaphoreType.DMA((4, 2, 2)),
            pltpu.SemaphoreType.DMA((4, 2, 2)),
            pltpu.SemaphoreType.DMA((SEQ + HEADS - 2,)),
            pltpu.SemaphoreType.DMA((SEQ + HEADS - 2,)),
        ],
        compiler_params=pltpu.CompilerParams(
            collective_id=0, has_side_effects=True, vmem_limit_bytes=48 * 1024 * 1024
        ),
    )(doc_lengths, queries, key_states, value_states)
    return pl.pallas_call(
        finish,
        out_shape=jax.ShapeDtypeStruct((rows, cols), jnp.bfloat16),
        in_specs=[pl.BlockSpec(memory_space=pltpu.VMEM)],
        out_specs=any_space,
        scratch_shapes=[vmem((rows, cols), jnp.bfloat16), pltpu.SemaphoreType.DMA((tiles,))],
        compiler_params=pltpu.CompilerParams(vmem_limit_bytes=12 * 1024 * 1024),
    )(acc)


def solution(mesh):
    return jax.shard_map(
        body,
        mesh=mesh,
        in_specs=(P(("seq", "head")), P("seq", "head"), P("seq", "head"), P("seq", "head")),
        out_specs=P("seq", "head"),
        check_vma=False,
    )
```

time: 74.4 us -> 57 us (0.77)
  Pallas kernels: 70.9 us -> 56.3 us
  local copies, waits for them, and re-layouts: 2.67 us -> 0 us
    pallas_call x1 -> x2, Pallas kernels: 70.9 us -> 56.3 us  [the longest x1 55 us: body(): pl.pallas_call(kernel, out_shape=vmem((tiles, 2, group_rows, 2 * HD), jnp...]
    unnamed x1 -> x0, local copies, waits for them, and re-layouts: 2.67 us -> none
where the time goes in v1:
time: 57 us
  Pallas kernels  56.3 us (99%)
  between operations  0.66 us (1%)
    pallas_call x1, Pallas kernels, body(): pl.pallas_call(kernel, out_shape=vmem((tiles, 2, group_rows, 2 * HD), jnp...  55 us
    pallas_call x1, Pallas kernels, body(): pl.pallas_call(finish, out_shape=jax.ShapeDtypeStruct((rows, cols), jnp.b...  1.26 us

profile of v1, /device:TPU:1, one launch (start us, length us, event | category | flops | bytes accessed | tf_op | source)
XLA Modules:
  0.0 57.0 jit_solution(15826036629377188921)
XLA Ops:
  0.7 55.0 %shard_map.46.acc = f32[6,2,512,256]{3,2,1,0:T(8,128)S(1)} custom-call(s32[1]{0:T(128)S(6)} %copy.5.len_ref, bf16[768,1024]{1,0:T(8,128)(2,1)} %q_hbm.1, bf16[768,128]{1,0:T(8,128)(2,1)} %k_hbm.1, bf16[768,128]{1,0:T(8,128)(2,1)} %v_hbm.1), custom_call_target="tpu_custom_call" | custom-call | tf_op jit(solution)/shard_map/pallas_call | solution.py:283
  55.7 1.3 %shard_map.47 = bf16[768,1024]{1,0:T(8,128)(2,1)} custom-call(f32[6,2,512,256]{3,2,1,0:T(8,128)S(1)} %shard_map.46.acc), custom_call_target="tpu_custom_call" | custom-call | tf_op jit(solution)/shard_map/pallas_call | solution.py:312
